TPU v7x, 256 devices: a whole 4x4x8 slice. The times are simulated.
256 devices in a mesh: dev: 128 (over y, x, z), rep: 2 (over core).
Axes of the slice: x: 4, y: 4, z: 8, core: 2. Of those that a mesh axis runs over, the one named last changes fastest.
Arguments:
- embeddings: float32 [32768, 4096], P(('rep', 'dev')), parts along dimension 0, may hold values from -130 to 130
- cluster_id: int32 [32768], P(('rep', 'dev')), parts along dimension 0, may hold values from 0 to 255, as said below
- member_order: int32 [32768], P(('rep', 'dev')), parts along dimension 0, may hold values from 0 to 127, as said below
- cluster_slot: int32 [512], P('rep'), parts along dimension 0, may hold values from 0 to 255, each once
- cluster_size: int32 [512], P('rep'), parts along dimension 0, may hold values from 16 to 128, as said below
Outputs:
- best_similarity: float32 [32768], P(('rep', 'dev')), parts along dimension 0
- keep: int32 [32768], P(('rep', 'dev')), parts along dimension 0
- cluster_mean: float32 [512], P(('rep', 'dev')), parts along dimension 0
There are 2 independent parts, one for each index of `rep`. A program takes and returns all parts, laid end to end along the dimension named above; each array names one. Nothing has to cross between parts.
Inputs may be any that keep to these rules, and one draw needn't show every extreme that they name: `cluster_id`: every cluster holds at most 128 rows and some cluster exactly 128. A cluster of n members has floor(n / 128) or ceil(n / 128) of them among the rows of each device, so at most 1, a number reached on every device. `member_order`: within a cluster of n members the ranks are 0 to n - 1, each once. `cluster_slot`: a permutation; cluster c is owned by device cluster_slot[c] // 2 of dev. `cluster_size`: the number of rows whose cluster_id is c.
All inputs are finite; a program needn't handle non-finite values.
Results may differ from a plain program's by a relative error of at most 0.0003.
Values may be sent and summed in bfloat16 or wider, within the bound.
A program may use at most 64 MiB of HBM per device.

v0:
```python
import jax
import jax.numpy as jnp
from jax import lax
from jax.sharding import PartitionSpec as P

CAP = 128


norm_eps = 1e-06
cutoff = 0.8


def normalized(values):
    squares_sum = jnp.sum(values * values, axis=1, keepdims=True)
    return (values * lax.rsqrt(squares_sum + norm_eps)).astype(jnp.bfloat16)


def block_best(row_units, col_units, is_live):
    similar = jnp.einsum("cid,cjd->cij", row_units, col_units, preferred_element_type=jnp.float32)
    count_rows = row_units.shape[1]
    count_cols = col_units.shape[1]
    row_pos = lax.broadcasted_iota(jnp.int32, (count_rows, count_cols), 0)
    col_pos = lax.broadcasted_iota(jnp.int32, (count_rows, count_cols), 1)
    allowed = (col_pos < row_pos)[None] & is_live[:, None, :count_cols]
    return jnp.max(jnp.where(allowed, similar, -1.0), axis=2)


def body(embeddings, cluster_id, member_order, cluster_slot, cluster_size):
    devices = lax.axis_size("dev")
    clusters = cluster_slot.shape[0]
    per_owner = clusters // devices
    row_count = embeddings.shape[0]
    capacity = CAP
    per_pair = capacity // devices
    columns = lax.broadcasted_iota(jnp.int32, (row_count, clusters), 1)
    member = cluster_id[:, None] == columns
    slot_row = jnp.sum(jnp.where(member, cluster_slot[None, :], 0), axis=1)
    earlier = (
        lax.broadcasted_iota(jnp.int32, (row_count, row_count), 1)
        < lax.broadcasted_iota(jnp.int32, (row_count, row_count), 0)
    ).astype(jnp.bfloat16)
    before = jnp.dot(earlier, member.astype(jnp.bfloat16), preferred_element_type=jnp.float32)
    row_rank = jnp.sum(jnp.where(member, before, 0.0), axis=1).astype(jnp.int32)
    send_place = slot_row * per_pair + row_rank
    source_row = (
        jnp.zeros((clusters * per_pair,), jnp.int32)
        .at[send_place]
        .set(jnp.arange(row_count, dtype=jnp.int32) + 1)
    )
    filled = source_row > 0
    row_pick = jnp.maximum(source_row - 1, 0)
    sent_order = jnp.where(filled, member_order[row_pick], -1)
    payload = normalized(embeddings)[row_pick]
    got_rows, got_order = (
        lax.all_to_all(payload, "dev", split_axis=0, concat_axis=0, tiled=True),
        lax.all_to_all(sent_order, "dev", split_axis=0, concat_axis=0, tiled=True),
    )
    slots_in = got_order.shape[0]
    local_cluster = jnp.arange(slots_in, dtype=jnp.int32) // per_pair % per_owner
    is_valid = got_order >= 0
    position = jnp.where(is_valid, local_cluster * capacity + got_order, per_owner * capacity)
    arrival = (
        jnp.zeros((per_owner * capacity,), jnp.int32)
        .at[position]
        .set(jnp.arange(slots_in, dtype=jnp.int32) + 1, mode="drop")
    )
    occupied = arrival > 0
    gathered = got_rows[jnp.maximum(arrival - 1, 0)]
    unit_rows = jnp.where(occupied[:, None], gathered, jnp.zeros((), jnp.bfloat16))
    unit_rows = unit_rows.reshape(per_owner, capacity, unit_rows.shape[1])
    owner_index = lax.axis_index("dev")
    my_slots = owner_index * per_owner + jnp.arange(per_owner, dtype=jnp.int32)
    own_match = cluster_slot[None, :] == my_slots[:, None]
    my_size = jnp.sum(jnp.where(own_match, cluster_size[None, :], 0), axis=1)
    spot_index = lax.broadcasted_iota(jnp.int32, (per_owner, capacity), 1)
    is_live = occupied.reshape(per_owner, capacity) & (spot_index < my_size[:, None])
    nearest = block_best(unit_rows, unit_rows, is_live)
    best_spot = jnp.where(is_live, nearest, -1.0)
    cluster_mean = jnp.sum(jnp.where(is_live, best_spot, 0.0), axis=1) / my_size.astype(jnp.float32)
    flat_best = best_spot.reshape(-1)
    answer = jnp.where(is_valid, flat_best[jnp.minimum(position, per_owner * capacity - 1)], 0.0)
    returned = lax.all_to_all(answer, "dev", split_axis=0, concat_axis=0, tiled=True)
    row_best = returned[send_place]
    keep_mask = (row_best < cutoff).astype(jnp.int32)
    return (row_best, keep_mask, cluster_mean)


def solution(mesh):
    placed = (P(("rep", "dev"), None), P(("rep", "dev")), P(("rep", "dev")), P("rep"), P("rep"))
    return jax.shard_map(
        body,
        mesh=mesh,
        in_specs=placed,
        out_specs=(P(("rep", "dev")), P(("rep", "dev")), P(("rep", "dev"))),
        check_vma=False,
    )
```

profile of v0, /device:TPU:2, one launch (start us, length us, event | category | flops | bytes accessed | tf_op | source)
XLA Modules:
  0.0 128.7 jit_solution(10026192653915958630)
XLA Ops:
  0.6 0.0 copy-start
  0.6 0.0 copy-start.1
  0.7 1.1 fusion.6
  1.8 0.9 select_reduce_fusion
  2.7 1.0 scatter_custom_fusion
  3.7 0.0 copy-done
  3.7 1.9 %gather_fusion = s32[256]{0:T(256)S(1)} fusion(s32[128]{0:T(128)S(1)} %copy-done, s32[1024]{0:T(1024)S(1)} %pad_clamp_fusion.3), kind=kCustom, calls=%fused_computation | custom fusion | bytes 3072 | tf_op jit(solution)/shard_map/gather | solution.py:52
  5.6 0.8 all_to_all.22
  6.4 15.4 %all-to-all-start = ((s32[128,2,1]{1,2,0:T(1,128)}), s32[128,2,1]{1,2,0:T(1,128)S(1)}, u32[]{:S(2)}, u32[]{:S(2)}) async-start(s32[128,2,1]{1,2,0:T(1,128)} %bitcast.2), calls=%async_computation | async-start | bytes 131072 | tf_op jit(solution)/shard_map/all_to_all | solution.py:56
  21.8 1.8 %multiply_reduce_fusion = f32[128]{0:T(128)S(1)} fusion(f32[128,4096]{1,0:T(8,128)} %param.5), kind=kLoop, calls=%fused_computation.10 | loop fusion | flops 1048448 | bytes 2097664 | tf_op jit(solution)/shard_map/reduce_sum | solution.py:14
  23.6 0.0 copy-done.1
  23.6 0.2 multiply_convert_fusion
  23.9 1.8 %gather_fusion.1 = bf16[256,4096]{1,0:T(8,128)(2,1)S(1)} fusion(bf16[128,4096]{1,0:T(8,128)(2,1)S(1)} %multiply_convert_fusion, s32[1024]{0:T(1024)S(1)} %pad_clamp_fusion.3), kind=kCustom, calls=%fused_computation.1 | custom fusion | bytes 4195328 | tf_op jit(solution)/shard_map/gather | solution.py:53
  25.7 2.7 %all_to_all.25 = bf16[128,2,4096]{2,1,0:T(2,128)(2,1)} reshape(bf16[256,4096]{1,0:T(8,128)(2,1)S(1)} %gather_fusion.1) | data formatting | bytes 4194304 | tf_op jit(solution)/shard_map/all_to_all | solution.py:55
  28.4 0.0 copy-start.2
  28.4 0.0 copy-start.3
  28.4 4.5 %all-to-all-done = s32[128,2,1]{1,2,0:T(1,128)S(1)} async-done(((s32[128,2,1]{1,2,0:T(1,128)}), s32[128,2,1]{1,2,0:T(1,128)S(1)}, u32[]{:S(2)}, u32[]{:S(2)}) %all-to-all-start) | async-done | bytes 1056 | tf_op jit(solution)/shard_map/all_to_all | solution.py:56
  32.9 9.9 %all-to-all-start.1 = ((bf16[128,2,4096]{2,1,0:T(2,128)(2,1)}), bf16[128,2,4096]{2,1,0:T(2,128)(2,1)}, u32[]{:S(2)}, u32[]{:S(2)}) async-start(bf16[128,2,4096]{2,1,0:T(2,128)(2,1)} %all_to_all.25), calls=%async_computation.1 | async-start | bytes 4194304 | tf_op jit(solution)/shard_map/all_to_all | solution.py:55
  42.9 0.0 copy-done.2
  42.9 0.0 copy-done.3
  42.9 0.2 fusion.12
  43.1 0.5 broadcast.262
  43.6 0.8 reduce.6
  44.4 0.1 all_to_all.24
  44.6 1.4 %scatter_custom_fusion.1 = s32[256]{0:T(256)S(1)} fusion(s32[256]{0:T(256)S(1)} %bitcast.24, s32[256]{0:T(256)S(1)} %iota_add_fusion, s32[]{:T(128)} %constant.27.clone.1), kind=kCustom, calls=%fused_computation.52 | custom fusion | bytes 1028 | tf_op jit(solution)/shard_map/scatter | solution.py:65
  46.0 0.1 fusion.17
  46.1 47.2 %all-to-all-done.1 = bf16[128,2,4096]{2,1,0:T(2,128)(2,1)} async-done(((bf16[128,2,4096]{2,1,0:T(2,128)(2,1)}), bf16[128,2,4096]{2,1,0:T(2,128)(2,1)}, u32[]{:S(2)}, u32[]{:S(2)}) %all-to-all-start.1) | async-done | bytes 2097184 | tf_op jit(solution)/shard_map/all_to_all | solution.py:55
  93.2 2.7 %all_to_all.27 = bf16[256,4096]{1,0:T(8,128)(2,1)S(1)} reshape(bf16[128,2,4096]{2,1,0:T(2,128)(2,1)} %all-to-all-done.1) | data formatting | bytes 4194304 | tf_op jit(solution)/shard_map/all_to_all | solution.py:55
  96.0 3.2 %gather_fusion.2 = bf16[256,4096]{1,0:T(8,128)(2,1)} fusion(bf16[256,4096]{1,0:T(8,128)(2,1)S(1)} %all_to_all.27, s32[1024]{0:T(1024)S(1)} %pad_clamp_fusion.2), kind=kCustom, calls=%fused_computation.2 | custom fusion | bytes 4195328 | tf_op jit(solution)/shard_map/gather | solution.py:68
  99.2 3.0 %fusion.7 = f32[2,128]{1,0:T(2,128)S(1)} fusion(bf16[2,128,4096]{2,1,0:T(8,128)(2,1)} %bitcast.21, pred[2,128]{1,0:T(4,128)(4,1)S(1)} %get-tuple-element.6, pred[2,128]{1,0:T(4,128)(4,1)S(1)} %get-tuple-element.5, pred[128,128]{0,1:T(8,128)(4,1)S(1)} %iota_compare_fusion.2), kind=kOutput, calls=%fused_computation.15 | convolution fusion | flops 269582080 | bytes 2115072 | tf_op jit(solution)/shard_map/cid,cjd->cij/dot_general | solution.py:19
  102.2 0.1 fusion.13
  102.3 0.1 fusion.14
  102.4 2.0 %gather_fusion.3 = f32[256]{0:T(256)S(1)} fusion(f32[256]{0:T(256)S(1)} %fusion.13, s32[1024]{0:T(1024)S(1)} %pad_clamp_fusion.1), kind=kCustom, calls=%fused_computation.3 | custom fusion | bytes 3072 | tf_op jit(solution)/shard_map/gather | solution.py:81
  104.4 0.1 gather.24
  104.5 0.6 compare_select_fusion
  105.1 9.1 %all-to-all-start.2 = ((f32[128,2,1]{1,2,0:T(1,128)}), f32[128,2,1]{1,2,0:T(1,128)S(1)}, u32[]{:S(2)}, u32[]{:S(2)}) async-start(f32[128,2,1]{1,2,0:T(1,128)} %bitcast.10), calls=%async_computation.2 | async-start | bytes 131072 | tf_op jit(solution)/shard_map/all_to_all | solution.py:82
  114.3 0.5 convert_divide_fusion
  114.8 10.6 %all-to-all-done.2 = f32[128,2,1]{1,2,0:T(1,128)S(1)} async-done(((f32[128,2,1]{1,2,0:T(1,128)}), f32[128,2,1]{1,2,0:T(1,128)S(1)}, u32[]{:S(2)}, u32[]{:S(2)}) %all-to-all-start.2) | async-done | bytes 1056 | tf_op jit(solution)/shard_map/all_to_all | solution.py:82
  125.4 0.5 broadcast.263
  125.9 0.8 reduce.7
  126.8 0.1 all_to_all.29
  126.9 1.3 gather_fusion.4
  128.2 0.0 copy-start.4
  128.2 0.5 compare_convert_fusion
  128.7 0.0 copy-done.4
  (15 shorter events, 0.1 us)
Async XLA Ops:
  0.6 3.1 %copy-start = (s32[128]{0:T(128)S(1)}, s32[128]{0:T(128)}, u32[]{:S(2)}) copy-start(s32[128]{0:T(128)} %param.7) | copy-start | bytes 1540
  0.6 23.0 %copy-start.1 = (f32[128,4096]{1,0:T(8,128)S(1)}, f32[128,4096]{1,0:T(8,128)}, u32[]{:S(2)}) copy-start(f32[128,4096]{1,0:T(8,128)} %param.5) | copy-start | bytes 6291460
  6.4 26.5 %all-to-all-start = ((s32[128,2,1]{1,2,0:T(1,128)}), s32[128,2,1]{1,2,0:T(1,128)S(1)}, u32[]{:S(2)}, u32[]{:S(2)}) async-start(s32[128,2,1]{1,2,0:T(1,128)} %bitcast.2), calls=%async_computation | async-start | bytes 131072 | tf_op jit(solution)/shard_map/all_to_all | solution.py:56
  28.4 14.5 %copy-start.2 = (s32[256]{0:T(256)S(1)}, s32[256]{0:T(256)}, u32[]{:S(2)}) copy-start(s32[256]{0:T(256)} %param.8) | copy-start | bytes 3076
  28.4 14.5 %copy-start.3 = (s32[256]{0:T(256)S(1)}, s32[256]{0:T(256)}, u32[]{:S(2)}) copy-start(s32[256]{0:T(256)} %param.9) | copy-start | bytes 3076
  32.9 60.3 %all-to-all-start.1 = ((bf16[128,2,4096]{2,1,0:T(2,128)(2,1)}), bf16[128,2,4096]{2,1,0:T(2,128)(2,1)}, u32[]{:S(2)}, u32[]{:S(2)}) async-start(bf16[128,2,4096]{2,1,0:T(2,128)(2,1)} %all_to_all.25), calls=%async_computation.1 | async-start | bytes 4194304 | tf_op jit(solution)/shard_map/all_to_all | solution.py:55
  105.1 20.3 %all-to-all-start.2 = ((f32[128,2,1]{1,2,0:T(1,128)}), f32[128,2,1]{1,2,0:T(1,128)S(1)}, u32[]{:S(2)}, u32[]{:S(2)}) async-start(f32[128,2,1]{1,2,0:T(1,128)} %bitcast.10), calls=%async_computation.2 | async-start | bytes 131072 | tf_op jit(solution)/shard_map/all_to_all | solution.py:82
  128.2 0.5 copy-start.4
where the time goes:
time: 129 us
  waiting for transfers between devices  62.3 us (48%)
  starting transfers between devices  34.5 us (27%)
  local copies, waits for them, and re-layouts  20.1 us (16%)
  other arithmetic  6.7 us (5%)
  matrix products  4.16 us (3%)
    all_to_all x1, waiting for transfers between devices, body(): lax.all_to_all(payload, 'dev', split_axis=0, concat_axis=0, tiled=True)  47.2 us
    all_to_all x1, starting transfers between devices, body(): lax.all_to_all(sent_order, 'dev', split_axis=0, concat_axis=0, tiled=True)  15.4 us
    all_to_all x1, waiting for transfers between devices, body(): lax.all_to_all(answer, 'dev', split_axis=0, concat_axis=0, tiled=True)  10.6 us
    all_to_all x1, starting transfers between devices, body(): lax.all_to_all(payload, 'dev', split_axis=0, concat_axis=0, tiled=True)  9.9 us
    all_to_all x1, starting transfers between devices, body(): lax.all_to_all(answer, 'dev', split_axis=0, concat_axis=0, tiled=True)  9.14 us
    all_to_all x2, local copies, waits for them, and re-layouts, body(): lax.all_to_all(payload, 'dev', split_axis=0, concat_axis=0, tiled=True)  5.4 us
    all_to_all x1, waiting for transfers between devices, body(): lax.all_to_all(sent_order, 'dev', split_axis=0, concat_axis=0, tiled=True)  4.51 us
    gather x1, local copies, waits for them, and re-layouts, body(): gathered = got_rows[jnp.maximum(arrival - 1, 0)]  3.2 us
  transfers between devices with their start and end apart: 3, of which 3 were waited for; matrix products, arithmetic and copies ran while one was open for 6% of the time, Pallas kernels for 0%

commit v1 on v0

v1 whole, which is shorter than its diff:
```python
import functools

import jax
import jax.numpy as jnp
from jax import lax
from jax.experimental import pallas as pl
from jax.experimental.pallas import tpu as pltpu
from jax.sharding import PartitionSpec as P

norm_eps = 1e-06
cutoff = 0.8
MESH = pl.DeviceIdType.MESH
NY, NX, NZ = 4, 4, 8
N = NY * NX * NZ
OFFSETS = [(i // (NX * NZ), i // NZ % NX, i % NZ) for i in range(N)]
TAG = 128


def shifted(me, dy, dx, dz):
    y, x, z = me // (NX * NZ), me // NZ % NX, me % NZ
    return (y + dy) % NY * (NX * NZ) + (x + dx) % NX * NZ + (z + dz) % NZ


def peer(me, i):
    return shifted(me, *OFFSETS[i])


def source(me, i):
    dy, dx, dz = OFFSETS[i]
    return shifted(me, NY - dy, NX - dx, NZ - dz)


def hops(i):
    return sum(min(d, n - d) for d, n in zip(OFFSETS[i], (NY, NX, NZ)))


FAR_FIRST = sorted(range(1, N), key=lambda i: -hops(i))
SEMS = N // NZ + NZ


def flag(i):
    return i // NZ if i >= NZ else N // NZ + i


def exchange(src, dst, send_sem, recv_sem, target):
    for i in FAR_FIRST:
        pair = pl.ds(2 * i, 2)
        pltpu.make_async_remote_copy(
            src.at[pair], dst.at[pair], send_sem.at[flag(i)], recv_sem.at[flag(i)],
            device_id={"dev": target(i)}, device_id_type=MESH,
        ).start()


def waits(src, dst, send_sem, recv_sem, target):
    for g in range(1, N // NZ):
        part = pl.ds(2 * NZ * g, 2 * NZ)
        yield pltpu.make_async_remote_copy(
            src.at[part], dst.at[part], send_sem.at[g], recv_sem.at[g],
            device_id={"dev": target(1)}, device_id_type=MESH,
        )
    for i in range(1, NZ):
        pair = pl.ds(2 * i, 2)
        yield pltpu.make_async_remote_copy(
            src.at[pair], dst.at[pair], send_sem.at[flag(i)], recv_sem.at[flag(i)],
            device_id={"dev": target(1)}, device_id_type=MESH,
        )


def kernel(emb_ref, id_hbm, order_hbm, slot_hbm, size_hbm, best_ref, keep_ref, mean_ref,
           id_ref, order_ref, slot_ref, size_ref, raw, unit, packed, got, answers, returned, load_sem, own_sem, send_sem, recv_sem, back_send, back_recv):
    me = lax.axis_index("dev")
    rows, width = raw.shape
    slots = packed.shape[0]
    pieces = 4
    step = rows // pieces
    smalls = []
    for p, (src, dst) in enumerate(
        ((id_hbm, id_ref), (slot_hbm, slot_ref), (order_hbm, order_ref), (size_hbm, size_ref))
    ):
        load = pltpu.make_async_copy(src, dst, load_sem.at[pieces + p])
        load.start()
        smalls.append(load)
    loads = []
    for p in range(pieces):
        part = pl.ds(p * step, step)
        load = pltpu.make_async_copy(emb_ref.at[part], raw.at[part], load_sem.at[p])
        load.start()
        loads.append(load)
    barrier = pltpu.get_barrier_semaphore()
    for i in FAR_FIRST:
        pl.semaphore_signal(barrier, inc=1, device_id={"dev": peer(me, i)}, device_id_type=MESH)

    for load in smalls:
        load.wait()
    member = lax.broadcasted_iota(jnp.int32, (slots, rows), 0) == id_ref[...]
    table = jnp.broadcast_to(slot_ref[...].astype(jnp.bfloat16), (8, slots))
    slot_row = jnp.dot(table, member.astype(jnp.bfloat16), preferred_element_type=jnp.float32)[0:1]
    slot_row = slot_row.astype(jnp.int32)
    place = lax.broadcasted_iota(jnp.int32, (slots, rows), 0)
    offset = place // 2
    goal = shifted(me, offset // (NX * NZ), offset // NZ % NX, offset % NZ)
    chosen = slot_row == goal * 2 + place % 2
    pick = chosen.astype(jnp.bfloat16)
    rank_next = (order_ref[...] + 1).astype(jnp.float32)
    tag = jnp.sum(jnp.where(chosen, rank_next, 0.0), axis=1, keepdims=True)
    packed[:, width:] = jnp.broadcast_to(tag, (slots, TAG)).astype(jnp.bfloat16)

    for p in range(pieces):
        loads[p].wait()
        part = pl.ds(p * step, step)
        values = raw[part]
        squares_sum = jnp.sum(values * values, axis=1, keepdims=True)
        unit[part] = (values * lax.rsqrt(squares_sum + norm_eps)).astype(jnp.bfloat16)
    chunk = 512
    for k in range(0, width, chunk):
        packed[:, k:k + chunk] = jnp.dot(
            pick, unit[:, k:k + chunk], preferred_element_type=jnp.float32
        ).astype(jnp.bfloat16)

    pl.semaphore_wait(barrier, N - 1)
    there = (packed, got, send_sem, recv_sem, functools.partial(peer, me))
    exchange(*there)
    own = pltpu.make_async_copy(packed.at[pl.ds(0, 2)], got.at[pl.ds(0, 2)], own_sem)
    own.start()
    own.wait()
    for copy in waits(*there):
        copy.wait_recv()

    similar = jnp.zeros((slots, slots), jnp.float32)
    chunk = 1024
    for k in range(0, width, chunk):
        block = got[:, k:k + chunk]
        similar += lax.dot_general(block, block, (((1,), (1,)), ((), ())), preferred_element_type=jnp.float32)
    tags = got[:, width:]
    first = (lax.broadcasted_iota(jnp.int32, (8, TAG), 1) == 0).astype(jnp.bfloat16)
    rank_j = lax.dot_general(first, tags, (((1,), (1,)), ((), ())), preferred_element_type=jnp.float32)[0:1]
    rank_i = tags[:, 0:1].astype(jnp.float32)
    sizes = [
        jnp.sum(jnp.where(slot_ref[...] == 2 * me + b, size_ref[...], 0), axis=1, keepdims=True).astype(jnp.float32)
        for b in range(2)
    ]
    side_i = lax.broadcasted_iota(jnp.int32, (slots, 1), 0) % 2
    side_j = lax.broadcasted_iota(jnp.int32, (1, slots), 1) % 2
    live_i = (rank_i > 0.0) & (rank_i <= jnp.where(side_i == 0, sizes[0], sizes[1]))
    live_j = (rank_j > 0.0) & (rank_j <= jnp.where(side_j == 0, sizes[0], sizes[1]))
    mark_j = jnp.where(live_j, rank_j, 1024.0)
    allowed = (side_i == side_j) & (mark_j < rank_i)
    nearest = jnp.max(jnp.where(allowed, similar, -1.0), axis=1, keepdims=True)
    best = jnp.where(live_i, nearest, -1.0)
    answers[...] = jnp.broadcast_to(best, answers.shape)

    back = (answers, returned, back_send, back_recv, functools.partial(source, me))
    exchange(*back)
    own = pltpu.make_async_copy(answers.at[pl.ds(0, 2)], returned.at[pl.ds(0, 2)], own_sem)
    own.start()
    lane = lax.broadcasted_iota(jnp.int32, (1, 128), 1)
    means = [
        jnp.sum(jnp.where(live_i & (side_i == b), best, 0.0), axis=0, keepdims=True) / sizes[b]
        for b in range(2)
    ]
    mean_ref[...] = jnp.where(lane == 0, means[0], means[1])
    own.wait()
    for copy in waits(*back):
        copy.wait_recv()
    row_best = jnp.max(jnp.where(chosen, returned[...], -2.0), axis=0, keepdims=True)
    best_ref[...] = row_best
    keep_ref[...] = (row_best < cutoff).astype(jnp.int32)
    for copy in (*waits(*there), *waits(*back)):
        copy.wait_send()


def body(embeddings, cluster_id, member_order, cluster_slot, cluster_size):
    rows, width = embeddings.shape
    clusters = cluster_slot.shape[0]
    slots = clusters
    vmem = pl.BlockSpec(memory_space=pltpu.VMEM)
    best, keep, mean = pl.pallas_call(
        kernel,
        out_shape=(
            jax.ShapeDtypeStruct((1, rows), jnp.float32),
            jax.ShapeDtypeStruct((1, rows), jnp.int32),
            jax.ShapeDtypeStruct((1, 128), jnp.float32),
        ),
        in_specs=[pl.BlockSpec(memory_space=pltpu.HBM)] * 5,
        out_specs=(vmem, vmem, vmem),
        scratch_shapes=[
            pltpu.VMEM((1, rows), jnp.int32),
            pltpu.VMEM((1, rows), jnp.int32),
            pltpu.VMEM((1, clusters), jnp.int32),
            pltpu.VMEM((1, clusters), jnp.int32),
            pltpu.VMEM((rows, width), jnp.float32),
            pltpu.VMEM((rows, width), jnp.bfloat16),
            pltpu.VMEM((slots, width + TAG), jnp.bfloat16),
            pltpu.VMEM((slots, width + TAG), jnp.bfloat16),
            pltpu.VMEM((slots, 128), jnp.float32),
            pltpu.VMEM((slots, 128), jnp.float32),
            pltpu.SemaphoreType.DMA((8,)),
            pltpu.SemaphoreType.DMA,
            pltpu.SemaphoreType.DMA((SEMS,)),
            pltpu.SemaphoreType.DMA((SEMS,)),
            pltpu.SemaphoreType.DMA((SEMS,)),
            pltpu.SemaphoreType.DMA((SEMS,)),
        ],
        compiler_params=pltpu.CompilerParams(collective_id=0, has_side_effects=True, vmem_limit_bytes=67_043_328),
    )(embeddings, cluster_id[None], member_order[None], cluster_slot[None], cluster_size[None])
    return best[0], keep[0], mean[0, : clusters // N]


def solution(mesh):
    placed = (P(("rep", "dev"), None), P(("rep", "dev")), P(("rep", "dev")), P("rep"), P("rep"))
    return jax.shard_map(
        body,
        mesh=mesh,
        in_specs=placed,
        out_specs=(P(("rep", "dev")), P(("rep", "dev")), P(("rep", "dev"))),
        check_vma=False,
    )
```

time: 129 us -> 75 us (0.58)
  Pallas kernels: 0 us -> 70.5 us
  waiting for transfers between devices: 62.3 us -> 0 us
  starting transfers between devices: 34.5 us -> 0 us
  local copies, waits for them, and re-layouts: 20.1 us -> 3.42 us
  other arithmetic: 6.7 us -> 0 us
  matrix products: 4.16 us -> 0 us
    pallas_call x0 -> x1, Pallas kernels: none -> 70.5 us  [body(): pl.pallas_call(kernel, out_shape=(jax.ShapeDtypeStruct((1, rows), jnp.flo...]
    all_to_all x3 -> x0, waiting for transfers between devices: 62.3 us -> none  [the longest x1 47.2 us: body(): lax.all_to_all(payload, 'dev', split_axis=0, concat_axis=0, tiled=True)]
    all_to_all x3 -> x0, starting transfers between devices: 34.5 us -> none  [the longest x1 15.4 us: body(): lax.all_to_all(sent_order, 'dev', split_axis=0, concat_axis=0, tiled=True)]
    gather x6 -> x0, local copies, waits for them, and re-layouts: 10.3 us -> none  [the longest x1 3.2 us: body(): gathered = got_rows[jnp.maximum(arrival - 1, 0)]]
    all_to_all x7 -> x0, local copies, waits for them, and re-layouts: 7.46 us -> none  [the longest x2 5.4 us: body(): lax.all_to_all(payload, 'dev', split_axis=0, concat_axis=0, tiled=True)]
    dot_general x2 -> x0, matrix products: 4.16 us -> none  [the longest x1 3.02 us: block_best(): jnp.einsum('cid,cjd->cij', row_units, col_units, preferred_element_type=j...]
    reduce_sum x4 -> x0, other arithmetic: 2.98 us -> none  [the longest x1 1.82 us: normalized(): squares_sum = jnp.sum(values * values, axis=1, keepdims=True)]
    scatter x2 -> x0, local copies, waits for them, and re-layouts: 2.37 us -> none  [the longest x1 1.4 us: body(): arrival = jnp.zeros((per_owner * capacity,), jnp.int32).at[position].set(...]
  transfers between devices with their start and end apart: 3 -> 0, of which waited for: 3 -> 0; matrix products, arithmetic and copies ran while one was open for 6% -> 0% of each run, Pallas kernels for 0% -> 0%
where the time goes in v1:
time: 75 us; the launch traced here: 74.5 us
  Pallas kernels  70.5 us (94%)
  local copies, waits for them, and re-layouts  3.42 us (5%)
    pallas_call x1, Pallas kernels, body(): pl.pallas_call(kernel, out_shape=(jax.ShapeDtypeStruct((1, rows), jnp.flo...  70.5 us
    unnamed x2, local copies, waits for them, and re-layouts  2.24 us

profile of v1, /device:TPU:2, one launch (start us, length us, event | category | flops | bytes accessed | tf_op | source)
XLA Modules:
  0.0 74.5 jit_solution(12650469072560104421)
XLA Ops:
  0.6 70.5 %shard_map.76 = (f32[1,128]{1,0:T(1,128)}, s32[1,128]{1,0:T(1,128)}, f32[1,128]{1,0:T(1,128)}) custom-call(f32[128,4096]{1,0:T(8,128)} %emb_ref.1, s32[1,128]{1,0:T(1,128)} %bitcast.10, s32[1,128]{1,0:T(1,128)} %bitcast.11, s32[1,256]{1,0:T(1,128)} %bitcast.8, s32[1,256]{1,0:T(1,128)} %bitcast.9), custom_call_target="tpu_custom_call" | custom-call | tf_op jit(solution)/shard_map/pallas_call | solution.py:177
  71.1 1.2 %slice_bitcast_fusion = f32[2]{0:T(128)} fusion(f32[1,128]{1,0:T(1,128)} %get-tuple-element.8), kind=kLoop, calls=%fused_computation | loop fusion | bytes 16 | tf_op jit(solution)/shard_map/squeeze | solution.py:206
  72.3 1.1 %copy.10 = f32[128]{0:T(128)} copy(f32[128]{0:T(128)} %bitcast.13) | data formatting | bytes 1024
  73.4 1.1 %copy.11 = s32[128]{0:T(128)} copy(s32[128]{0:T(128)} %bitcast.12) | data formatting | bytes 1024

commit v2 on v1

--- a/solution.py
+++ b/solution.py
@@ -42,32 +42,32 @@
     return i // NZ if i >= NZ else N // NZ + i
 
 
-def exchange(src, dst, send_sem, recv_sem, target):
+def exchange(src, dst, send_sem, recv_sem, target, unit):
     for i in FAR_FIRST:
-        pair = pl.ds(2 * i, 2)
+        pair = pl.ds(unit * i, unit)
         pltpu.make_async_remote_copy(
             src.at[pair], dst.at[pair], send_sem.at[flag(i)], recv_sem.at[flag(i)],
             device_id={"dev": target(i)}, device_id_type=MESH,
         ).start()
 
 
-def waits(src, dst, send_sem, recv_sem, target):
+def waits(src, dst, send_sem, recv_sem, target, unit):
     for g in range(1, N // NZ):
-        part = pl.ds(2 * NZ * g, 2 * NZ)
+        part = pl.ds(unit * NZ * g, unit * NZ)
         yield pltpu.make_async_remote_copy(
             src.at[part], dst.at[part], send_sem.at[g], recv_sem.at[g],
             device_id={"dev": target(1)}, device_id_type=MESH,
         )
     for i in range(1, NZ):
-        pair = pl.ds(2 * i, 2)
+        pair = pl.ds(unit * i, unit)
         yield pltpu.make_async_remote_copy(
             src.at[pair], dst.at[pair], send_sem.at[flag(i)], recv_sem.at[flag(i)],
             device_id={"dev": target(1)}, device_id_type=MESH,
         )
 
 
-def kernel(emb_ref, id_hbm, order_hbm, slot_hbm, size_hbm, best_ref, keep_ref, mean_ref,
-           id_ref, order_ref, slot_ref, size_ref, raw, unit, packed, got, answers, returned, load_sem, own_sem, send_sem, recv_sem, back_send, back_recv):
+def kernel(emb_ref, id_hbm, order_hbm, slot_hbm, size_hbm, best_ref, mean_ref,
+           id_ref, order_ref, slot_ref, size_ref, raw, unit, packed, got, spread, answers, returned, load_sem, own_sem, send_sem, recv_sem, back_send, back_recv):
     me = lax.axis_index("dev")
     rows, width = raw.shape
     slots = packed.shape[0]
@@ -118,7 +118,7 @@
         ).astype(jnp.bfloat16)
 
     pl.semaphore_wait(barrier, N - 1)
-    there = (packed, got, send_sem, recv_sem, functools.partial(peer, me))
+    there = (packed, got, send_sem, recv_sem, functools.partial(peer, me), 2)
     exchange(*there)
     own = pltpu.make_async_copy(packed.at[pl.ds(0, 2)], got.at[pl.ds(0, 2)], own_sem)
     own.start()
@@ -147,13 +147,15 @@
     allowed = (side_i == side_j) & (mark_j < rank_i)
     nearest = jnp.max(jnp.where(allowed, similar, -1.0), axis=1, keepdims=True)
     best = jnp.where(live_i, nearest, -1.0)
-    answers[...] = jnp.broadcast_to(best, answers.shape)
-
-    back = (answers, returned, back_send, back_recv, functools.partial(source, me))
+    spread[...] = jnp.broadcast_to(best, spread.shape)
+    halves = [spread[pl.ds(b, N, stride=2), :] for b in range(2)]
+    lane = lax.broadcasted_iota(jnp.int32, (1, 128), 1)
+    answers[...] = jnp.where(lane < 64, halves[0], halves[1])
+
+    back = (answers, returned, back_send, back_recv, functools.partial(source, me), 1)
     exchange(*back)
-    own = pltpu.make_async_copy(answers.at[pl.ds(0, 2)], returned.at[pl.ds(0, 2)], own_sem)
+    own = pltpu.make_async_copy(answers.at[pl.ds(0, 1)], returned.at[pl.ds(0, 1)], own_sem)
     own.start()
-    lane = lax.broadcasted_iota(jnp.int32, (1, 128), 1)
     means = [
         jnp.sum(jnp.where(live_i & (side_i == b), best, 0.0), axis=0, keepdims=True) / sizes[b]
         for b in range(2)
@@ -162,11 +164,22 @@
     own.wait()
     for copy in waits(*back):
         copy.wait_recv()
-    row_best = jnp.max(jnp.where(chosen, returned[...], -2.0), axis=0, keepdims=True)
+    offset = lax.broadcasted_iota(jnp.int32, (N, rows), 0)
+    goal = shifted(me, offset // (NX * NZ), offset // NZ % NX, offset % NZ)
+    row_best = jnp.full((1, rows), -2.0, jnp.float32)
+    for b in range(2):
+        found = jnp.where(slot_row == 2 * goal + b, returned[:, 64 * b:64 * b + 1], -2.0)
+        row_best = jnp.maximum(row_best, jnp.max(found, axis=0, keepdims=True))
     best_ref[...] = row_best
-    keep_ref[...] = (row_best < cutoff).astype(jnp.int32)
     for copy in (*waits(*there), *waits(*back)):
         copy.wait_send()
+
+
+def finish(best_ref, mean_ref, row_ref, keep_ref, cluster_ref):
+    best = best_ref[0]
+    row_ref[...] = best
+    keep_ref[...] = (best < cutoff).astype(jnp.int32)
+    cluster_ref[...] = mean_ref[0, : cluster_ref.shape[0]]
 
 
 def body(embeddings, cluster_id, member_order, cluster_slot, cluster_size):
@@ -174,15 +187,14 @@
     clusters = cluster_slot.shape[0]
     slots = clusters
     vmem = pl.BlockSpec(memory_space=pltpu.VMEM)
-    best, keep, mean = pl.pallas_call(
+    best, mean = pl.pallas_call(
         kernel,
         out_shape=(
             jax.ShapeDtypeStruct((1, rows), jnp.float32),
-            jax.ShapeDtypeStruct((1, rows), jnp.int32),
             jax.ShapeDtypeStruct((1, 128), jnp.float32),
         ),
         in_specs=[pl.BlockSpec(memory_space=pltpu.HBM)] * 5,
-        out_specs=(vmem, vmem, vmem),
+        out_specs=(vmem, vmem),
         scratch_shapes=[
             pltpu.VMEM((1, rows), jnp.int32),
             pltpu.VMEM((1, rows), jnp.int32),
@@ -193,7 +205,8 @@
             pltpu.VMEM((slots, width + TAG), jnp.bfloat16),
             pltpu.VMEM((slots, width + TAG), jnp.bfloat16),
             pltpu.VMEM((slots, 128), jnp.float32),
-            pltpu.VMEM((slots, 128), jnp.float32),
+            pltpu.VMEM((N, 128), jnp.float32),
+            pltpu.VMEM((N, 128), jnp.float32),
             pltpu.SemaphoreType.DMA((8,)),
             pltpu.SemaphoreType.DMA,
             pltpu.SemaphoreType.DMA((SEMS,)),
@@ -203,7 +216,16 @@
         ],
         compiler_params=pltpu.CompilerParams(collective_id=0, has_side_effects=True, vmem_limit_bytes=67_043_328),
     )(embeddings, cluster_id[None], member_order[None], cluster_slot[None], cluster_size[None])
-    return best[0], keep[0], mean[0, : clusters // N]
+    return pl.pallas_call(
+        finish,
+        out_shape=(
+            jax.ShapeDtypeStruct((rows,), jnp.float32),
+            jax.ShapeDtypeStruct((rows,), jnp.int32),
+            jax.ShapeDtypeStruct((clusters // N,), jnp.float32),
+        ),
+        in_specs=[vmem, vmem],
+        out_specs=(vmem, vmem, vmem),
+    )(best, mean)
 
 
 def solution(mesh):

time: 75 us -> 72.5 us (0.967)
  local copies, waits for them, and re-layouts: 3.42 us -> 0 us
  Pallas kernels: 70.5 us -> 71.6 us
    unnamed x2 -> x0, local copies, waits for them, and re-layouts: 2.24 us -> none
    squeeze x1 -> x0, local copies, waits for them, and re-layouts: 1.18 us -> none  [body(): return (best[0], keep[0], mean[0, :clusters // N])]
    pallas_call x0 -> x1, Pallas kernels: none -> 1.15 us  [body(): pl.pallas_call(finish, out_shape=(jax.ShapeDtypeStruct((rows,), jnp.float...]
where the time goes in v2:
time: 72.5 us; the launch traced here: 72.3 us
  Pallas kernels  71.6 us (99%)
    pallas_call x1, Pallas kernels, body(): pl.pallas_call(kernel, out_shape=(jax.ShapeDtypeStruct((1, rows), jnp.flo...  70.5 us

profile of v2, /device:TPU:2, one launch (start us, length us, event | category | flops | bytes accessed | tf_op | source)
XLA Modules:
  0.0 72.3 jit_solution(13828376745018545760)
XLA Ops:
  0.6 70.5 %shard_map.76 = (f32[1,128]{1,0:T(1,128)}, f32[1,128]{1,0:T(1,128)}) custom-call(f32[128,4096]{1,0:T(8,128)} %emb_ref.1, s32[1,128]{1,0:T(1,128)} %bitcast.6, s32[1,128]{1,0:T(1,128)} %bitcast.7, s32[1,256]{1,0:T(1,128)} %bitcast.4, s32[1,256]{1,0:T(1,128)} %bitcast.5), custom_call_target="tpu_custom_call" | custom-call | tf_op jit(solution)/shard_map/pallas_call | solution.py:190
  71.1 1.2 %shard_map.77 = (f32[128]{0:T(128)}, s32[128]{0:T(128)}, f32[2]{0:T(128)}) custom-call(f32[1,128]{1,0:T(1,128)} %get-tuple-element.5.best_ref, f32[1,128]{1,0:T(1,128)} %get-tuple-element.6.mean_ref), custom_call_target="tpu_custom_call" | custom-call | tf_op jit(solution)/shard_map/pallas_call | solution.py:219

commit v3 on v2

--- a/solution.py
+++ b/solution.py
@@ -30,11 +30,14 @@
     return shifted(me, NY - dy, NX - dx, NZ - dz)
 
 
-def hops(i):
-    return sum(min(d, n - d) for d, n in zip(OFFSETS[i], (NY, NX, NZ)))
-
-
-FAR_FIRST = sorted(range(1, N), key=lambda i: -hops(i))
+ORDER = [
+    i
+    for dy in (2, 3, 1, 0)
+    for dx in (2, 1, 3, 0)
+    for dz in (4, 3, 5, 2, 6, 1, 7, 0)
+    for i in [(dy * NX + dx) * NZ + dz]
+    if i
+]
 SEMS = N // NZ + NZ
 
 
@@ -43,7 +46,7 @@
 
 
 def exchange(src, dst, send_sem, recv_sem, target, unit):
-    for i in FAR_FIRST:
+    for i in ORDER:
         pair = pl.ds(unit * i, unit)
         pltpu.make_async_remote_copy(
             src.at[pair], dst.at[pair], send_sem.at[flag(i)], recv_sem.at[flag(i)],
@@ -51,14 +54,16 @@
         ).start()
 
 
-def waits(src, dst, send_sem, recv_sem, target, unit):
-    for g in range(1, N // NZ):
+def waits(src, dst, send_sem, recv_sem, target, unit, groups=range(N // NZ)):
+    for g in groups:
+        if g == 0:
+            continue
         part = pl.ds(unit * NZ * g, unit * NZ)
         yield pltpu.make_async_remote_copy(
             src.at[part], dst.at[part], send_sem.at[g], recv_sem.at[g],
             device_id={"dev": target(1)}, device_id_type=MESH,
         )
-    for i in range(1, NZ):
+    for i in range(1, NZ) if 0 in groups else ():
         pair = pl.ds(unit * i, unit)
         yield pltpu.make_async_remote_copy(
             src.at[pair], dst.at[pair], send_sem.at[flag(i)], recv_sem.at[flag(i)],
@@ -87,7 +92,7 @@
         load.start()
         loads.append(load)
     barrier = pltpu.get_barrier_semaphore()
-    for i in FAR_FIRST:
+    for i in ORDER:
         pl.semaphore_signal(barrier, inc=1, device_id={"dev": peer(me, i)}, device_id_type=MESH)
 
     for load in smalls:
@@ -123,30 +128,68 @@
     own = pltpu.make_async_copy(packed.at[pl.ds(0, 2)], got.at[pl.ds(0, 2)], own_sem)
     own.start()
     own.wait()
-    for copy in waits(*there):
-        copy.wait_recv()
-
-    similar = jnp.zeros((slots, slots), jnp.float32)
-    chunk = 1024
-    for k in range(0, width, chunk):
-        block = got[:, k:k + chunk]
-        similar += lax.dot_general(block, block, (((1,), (1,)), ((), ())), preferred_element_type=jnp.float32)
-    tags = got[:, width:]
-    first = (lax.broadcasted_iota(jnp.int32, (8, TAG), 1) == 0).astype(jnp.bfloat16)
-    rank_j = lax.dot_general(first, tags, (((1,), (1,)), ((), ())), preferred_element_type=jnp.float32)[0:1]
-    rank_i = tags[:, 0:1].astype(jnp.float32)
     sizes = [
         jnp.sum(jnp.where(slot_ref[...] == 2 * me + b, size_ref[...], 0), axis=1, keepdims=True).astype(jnp.float32)
         for b in range(2)
     ]
+    first = (lax.broadcasted_iota(jnp.int32, (8, TAG), 1) == 0).astype(jnp.bfloat16)
+
+    def arrive(groups):
+        for copy in waits(*there, groups):
+            copy.wait_recv()
+
+    def gram(start, count, start_j, count_j):
+        total = jnp.zeros((count, count_j), jnp.float32)
+        chunk = 1024
+        for k in range(0, width, chunk):
+            total += lax.dot_general(
+                got[start:start + count, k:k + chunk], got[start_j:start_j + count_j, k:k + chunk],
+                (((1,), (1,)), ((), ())), preferred_element_type=jnp.float32,
+            )
+        return total
+
+    def rows_of(start, count):
+        rank = got[start:start + count, width:][:, 0:1].astype(jnp.float32)
+        side = lax.broadcasted_iota(jnp.int32, (count, 1), 0) % 2
+        live = (rank > 0.0) & (rank <= jnp.where(side == 0, sizes[0], sizes[1]))
+        return jnp.where(live, rank, -1.0), side
+
+    def columns_of(start, count):
+        rank = lax.dot_general(
+            first, got[start:start + count, width:], (((1,), (1,)), ((), ())), preferred_element_type=jnp.float32
+        )[0:1]
+        side = lax.broadcasted_iota(jnp.int32, (1, count), 1) % 2
+        live = (rank > 0.0) & (rank <= jnp.where(side == 0, sizes[0], sizes[1]))
+        return jnp.where(live, rank, 1024.0), side
+
+    def nearest(similar, row, column):
+        allowed = (row[1] == column[1]) & (column[0] < row[0])
+        return jnp.max(jnp.where(allowed, similar, -1.0), axis=1, keepdims=True)
+
+    low, mid, high = (0, slots // 4), (slots // 4, slots // 4), (slots // 2, slots // 2)
+    arrive(range(8, 16))
+    row_c, column_c = rows_of(*high), columns_of(*high)
+    best_c = nearest(gram(*high, *high), row_c, column_c)
+    arrive(range(4, 8))
+    row_b, column_b = rows_of(*mid), columns_of(*mid)
+    best_b = nearest(gram(*mid, *mid), row_b, column_b)
+    across = gram(*mid, *high)
+    best_b = jnp.maximum(best_b, nearest(across, row_b, column_c))
+    best_c = jnp.maximum(best_c, nearest(across.T, row_c, column_b))
+    arrive(range(4))
+    row_a, column_a = rows_of(*low), columns_of(*low)
+    last = gram(*low, 0, slots)
+    best_a = jnp.maximum(
+        nearest(last[:, :slots // 2], row_a, columns_of(0, slots // 2)),
+        nearest(last[:, slots // 2:], row_a, column_c),
+    )
+    turned = last.T
+    best_b = jnp.maximum(best_b, nearest(turned[slots // 4:slots // 2], row_b, column_a))
+    best_c = jnp.maximum(best_c, nearest(turned[slots // 2:], row_c, column_a))
+    best = jnp.concatenate([best_a, best_b, best_c], axis=0)
+    rank_i = jnp.concatenate([row_a[0], row_b[0], row_c[0]], axis=0)
+    live_i = rank_i > 0.0
     side_i = lax.broadcasted_iota(jnp.int32, (slots, 1), 0) % 2
-    side_j = lax.broadcasted_iota(jnp.int32, (1, slots), 1) % 2
-    live_i = (rank_i > 0.0) & (rank_i <= jnp.where(side_i == 0, sizes[0], sizes[1]))
-    live_j = (rank_j > 0.0) & (rank_j <= jnp.where(side_j == 0, sizes[0], sizes[1]))
-    mark_j = jnp.where(live_j, rank_j, 1024.0)
-    allowed = (side_i == side_j) & (mark_j < rank_i)
-    nearest = jnp.max(jnp.where(allowed, similar, -1.0), axis=1, keepdims=True)
-    best = jnp.where(live_i, nearest, -1.0)
     spread[...] = jnp.broadcast_to(best, spread.shape)
     halves = [spread[pl.ds(b, N, stride=2), :] for b in range(2)]
     lane = lax.broadcasted_iota(jnp.int32, (1, 128), 1)
@@ -189,10 +232,7 @@
     vmem = pl.BlockSpec(memory_space=pltpu.VMEM)
     best, mean = pl.pallas_call(
         kernel,
-        out_shape=(
-            jax.ShapeDtypeStruct((1, rows), jnp.float32),
-            jax.ShapeDtypeStruct((1, 128), jnp.float32),
-        ),
+        out_shape=(pltpu.VMEM((1, rows), jnp.float32), pltpu.VMEM((1, 128), jnp.float32)),
         in_specs=[pl.BlockSpec(memory_space=pltpu.HBM)] * 5,
         out_specs=(vmem, vmem),
         scratch_shapes=[
@@ -214,8 +254,11 @@
             pltpu.SemaphoreType.DMA((SEMS,)),
             pltpu.SemaphoreType.DMA((SEMS,)),
         ],
-        compiler_params=pltpu.CompilerParams(collective_id=0, has_side_effects=True, vmem_limit_bytes=67_043_328),
-    )(embeddings, cluster_id[None], member_order[None], cluster_slot[None], cluster_size[None])
+        compiler_params=pltpu.CompilerParams(collective_id=0, has_side_effects=True, vmem_limit_bytes=32 * 1024 * 1024),
+    )(*(
+        pltpu.with_memory_space_constraint(x, pltpu.HBM)
+        for x in (embeddings, cluster_id[None], member_order[None], cluster_slot[None], cluster_size[None])
+    ))
     return pl.pallas_call(
         finish,
         out_shape=(
@@ -225,7 +268,8 @@
         ),
         in_specs=[vmem, vmem],
         out_specs=(vmem, vmem, vmem),
-    )(best, mean)
+        compiler_params=pltpu.CompilerParams(vmem_limit_bytes=1024 * 1024),
+    )(pltpu.with_memory_space_constraint(best, pltpu.VMEM), pltpu.with_memory_space_constraint(mean, pltpu.VMEM))
 
 
 def solution(mesh):

time: 72.5 us -> 70.7 us (0.975)
  Pallas kernels: 71.6 us -> 69.9 us
    pallas_call x1, Pallas kernels: 70.5 us -> 69.3 us  [body(): pl.pallas_call(kernel, out_shape=(pltpu.VMEM((1, rows), jnp.float32), plt...]
where the time goes in v3:
time: 70.7 us; the launch traced here: 70.5 us
  Pallas kernels  69.9 us (99%)
    pallas_call x1, Pallas kernels, body(): pl.pallas_call(kernel, out_shape=(pltpu.VMEM((1, rows), jnp.float32), plt...  69.3 us

profile of v3, /device:TPU:2, one launch (start us, length us, event | category | flops | bytes accessed | tf_op | source)
XLA Modules:
  0.0 70.5 jit_solution(11168300072520236700)
XLA Ops:
  0.6 69.3 %shard_map.76 = (f32[1,128]{1,0:T(1,128)S(1)}, f32[1,128]{1,0:T(1,128)S(1)}) custom-call(f32[128,4096]{1,0:T(8,128)} %emb_ref.1, s32[1,128]{1,0:T(1,128)} %bitcast.6, s32[1,128]{1,0:T(1,128)} %bitcast.7, s32[1,256]{1,0:T(1,128)} %bitcast.4, s32[1,256]{1,0:T(1,128)} %bitcast.5), custom_call_target="tpu_custom_call" | custom-call | tf_op jit(solution)/shard_map/pallas_call | solution.py:233
  70.0 0.5 shard_map.77

commit v4 on v3

--- a/solution.py
+++ b/solution.py
@@ -13,7 +13,6 @@
 NY, NX, NZ = 4, 4, 8
 N = NY * NX * NZ
 OFFSETS = [(i // (NX * NZ), i // NZ % NX, i % NZ) for i in range(N)]
-TAG = 128
 
 
 def shifted(me, dy, dx, dz):
@@ -45,8 +44,8 @@
     return i // NZ if i >= NZ else N // NZ + i
 
 
-def exchange(src, dst, send_sem, recv_sem, target, unit):
-    for i in ORDER:
+def exchange(src, dst, send_sem, recv_sem, target, unit, order=ORDER):
+    for i in order:
         pair = pl.ds(unit * i, unit)
         pltpu.make_async_remote_copy(
             src.at[pair], dst.at[pair], send_sem.at[flag(i)], recv_sem.at[flag(i)],
@@ -72,7 +71,8 @@
 
 
 def kernel(emb_ref, id_hbm, order_hbm, slot_hbm, size_hbm, best_ref, mean_ref,
-           id_ref, order_ref, slot_ref, size_ref, raw, unit, packed, got, spread, answers, returned, load_sem, own_sem, send_sem, recv_sem, back_send, back_recv):
+           id_ref, order_ref, slot_ref, size_ref, raw, unit, packed, got, ranks, spoken, column, heard, spread, answers, returned, load_sem, own_sem, send_sem, recv_sem,
+           back_send, back_recv, speak_send, speak_recv, pass_send, pass_recv):
     me = lax.axis_index("dev")
     rows, width = raw.shape
     slots = packed.shape[0]
@@ -107,8 +107,17 @@
     chosen = slot_row == goal * 2 + place % 2
     pick = chosen.astype(jnp.bfloat16)
     rank_next = (order_ref[...] + 1).astype(jnp.float32)
-    tag = jnp.sum(jnp.where(chosen, rank_next, 0.0), axis=1, keepdims=True)
-    packed[:, width:] = jnp.broadcast_to(tag, (slots, TAG)).astype(jnp.bfloat16)
+    said = lax.dot_general(
+        jnp.broadcast_to(rank_next, (8, rows)).astype(jnp.bfloat16), pick, (((1,), (1,)), ((), ())),
+        preferred_element_type=jnp.float32,
+    )
+    slot_lane = lax.broadcasted_iota(jnp.int32, (NZ, slots), 1)
+    said = jnp.where(slot_lane // 2 % NZ == lax.broadcasted_iota(jnp.int32, (NZ, slots), 0), said, 0.0)
+    slot_line = lax.broadcasted_iota(jnp.int32, (slots, 128), 0)
+    fold = lax.broadcasted_iota(jnp.int32, (slots, 128), 1) == slot_line // (2 * NZ) * 2 + slot_line % 2
+    said = jnp.dot(said.astype(jnp.bfloat16), fold.astype(jnp.bfloat16), preferred_element_type=jnp.float32)
+    spoken[...] = said
+    column[0:1] = said[0:1]
 
     for p in range(pieces):
         loads[p].wait()
@@ -124,7 +133,29 @@
 
     pl.semaphore_wait(barrier, N - 1)
     there = (packed, got, send_sem, recv_sem, functools.partial(peer, me), 2)
-    exchange(*there)
+    speak = [
+        pltpu.make_async_remote_copy(
+            spoken.at[pl.ds(dz, 1)], column.at[pl.ds(dz, 1)], speak_send.at[dz], speak_recv.at[dz],
+            device_id={"dev": shifted(me, 0, 0, dz)}, device_id_type=MESH,
+        )
+        for dz in range(1, NZ)
+    ]
+    for copy in speak:
+        copy.start()
+    early = len(ORDER) // 4
+    exchange(*there, ORDER[:early])
+    for copy in speak:
+        copy.wait_recv()
+    forward = [
+        pltpu.make_async_remote_copy(
+            column, heard.at[q], pass_send.at[q], pass_recv.at[q],
+            device_id={"dev": shifted(me, q // NX, q % NX, 0)}, device_id_type=MESH,
+        )
+        for q in range(1, NY * NX)
+    ]
+    for copy in forward:
+        copy.start()
+    exchange(*there, ORDER[early:])
     own = pltpu.make_async_copy(packed.at[pl.ds(0, 2)], got.at[pl.ds(0, 2)], own_sem)
     own.start()
     own.wait()
@@ -132,7 +163,15 @@
         jnp.sum(jnp.where(slot_ref[...] == 2 * me + b, size_ref[...], 0), axis=1, keepdims=True).astype(jnp.float32)
         for b in range(2)
     ]
-    first = (lax.broadcasted_iota(jnp.int32, (8, TAG), 1) == 0).astype(jnp.bfloat16)
+    heard[0] = column[...]
+    for copy in forward:
+        copy.wait_recv()
+    told = heard[...].reshape(N, 128)
+    told_line = lax.broadcasted_iota(jnp.int32, (N, 128), 0) // NZ * 2
+    told_lane = lax.broadcasted_iota(jnp.int32, (N, 128), 1)
+    for b in range(2):
+        rank = jnp.sum(jnp.where(told_lane == told_line + b, told, 0.0), axis=1, keepdims=True)
+        ranks[pl.ds(b, N, stride=2), :] = jnp.broadcast_to(rank, (N, 128))
 
     def arrive(groups):
         for copy in waits(*there, groups):
@@ -149,15 +188,13 @@
         return total
 
     def rows_of(start, count):
-        rank = got[start:start + count, width:][:, 0:1].astype(jnp.float32)
+        rank = ranks[start:start + count, 0:1]
         side = lax.broadcasted_iota(jnp.int32, (count, 1), 0) % 2
         live = (rank > 0.0) & (rank <= jnp.where(side == 0, sizes[0], sizes[1]))
         return jnp.where(live, rank, -1.0), side
 
     def columns_of(start, count):
-        rank = lax.dot_general(
-            first, got[start:start + count, width:], (((1,), (1,)), ((), ())), preferred_element_type=jnp.float32
-        )[0:1]
+        rank = ranks[start:start + count, :].T[0:1]
         side = lax.broadcasted_iota(jnp.int32, (1, count), 1) % 2
         live = (rank > 0.0) & (rank <= jnp.where(side == 0, sizes[0], sizes[1]))
         return jnp.where(live, rank, 1024.0), side
@@ -167,20 +204,21 @@
         return jnp.max(jnp.where(allowed, similar, -1.0), axis=1, keepdims=True)
 
     low, mid, high = (0, slots // 4), (slots // 4, slots // 4), (slots // 2, slots // 2)
+    row_a, column_a = rows_of(*low), columns_of(*low)
+    row_b, column_b = rows_of(*mid), columns_of(*mid)
+    row_c, column_c = rows_of(*high), columns_of(*high)
+    column_ab = columns_of(0, slots // 2)
     arrive(range(8, 16))
-    row_c, column_c = rows_of(*high), columns_of(*high)
     best_c = nearest(gram(*high, *high), row_c, column_c)
     arrive(range(4, 8))
-    row_b, column_b = rows_of(*mid), columns_of(*mid)
     best_b = nearest(gram(*mid, *mid), row_b, column_b)
     across = gram(*mid, *high)
     best_b = jnp.maximum(best_b, nearest(across, row_b, column_c))
     best_c = jnp.maximum(best_c, nearest(across.T, row_c, column_b))
     arrive(range(4))
-    row_a, column_a = rows_of(*low), columns_of(*low)
     last = gram(*low, 0, slots)
     best_a = jnp.maximum(
-        nearest(last[:, :slots // 2], row_a, columns_of(0, slots // 2)),
+        nearest(last[:, :slots // 2], row_a, column_ab),
         nearest(last[:, slots // 2:], row_a, column_c),
     )
     turned = last.T
@@ -214,7 +252,7 @@
         found = jnp.where(slot_row == 2 * goal + b, returned[:, 64 * b:64 * b + 1], -2.0)
         row_best = jnp.maximum(row_best, jnp.max(found, axis=0, keepdims=True))
     best_ref[...] = row_best
-    for copy in (*waits(*there), *waits(*back)):
+    for copy in (*waits(*there), *waits(*back), *speak, *forward):
         copy.wait_send()
 
 
@@ -242,8 +280,12 @@
             pltpu.VMEM((1, clusters), jnp.int32),
             pltpu.VMEM((rows, width), jnp.float32),
             pltpu.VMEM((rows, width), jnp.bfloat16),
-            pltpu.VMEM((slots, width + TAG), jnp.bfloat16),
-            pltpu.VMEM((slots, width + TAG), jnp.bfloat16),
+            pltpu.VMEM((slots, width), jnp.bfloat16),
+            pltpu.VMEM((slots, width), jnp.bfloat16),
+            pltpu.VMEM((slots, 128), jnp.float32),
+            pltpu.VMEM((NZ, 128), jnp.float32),
+            pltpu.VMEM((NZ, 128), jnp.float32),
+            pltpu.VMEM((NY * NX, NZ, 128), jnp.float32),
             pltpu.VMEM((slots, 128), jnp.float32),
             pltpu.VMEM((N, 128), jnp.float32),
             pltpu.VMEM((N, 128), jnp.float32),
@@ -253,6 +295,10 @@
             pltpu.SemaphoreType.DMA((SEMS,)),
             pltpu.SemaphoreType.DMA((SEMS,)),
             pltpu.SemaphoreType.DMA((SEMS,)),
+            pltpu.SemaphoreType.DMA((NZ,)),
+            pltpu.SemaphoreType.DMA((NZ,)),
+            pltpu.SemaphoreType.DMA((NY * NX,)),
+            pltpu.SemaphoreType.DMA((NY * NX,)),
         ],
         compiler_params=pltpu.CompilerParams(collective_id=0, has_side_effects=True, vmem_limit_bytes=32 * 1024 * 1024),
     )(*(

time: 70.7 us -> 69.8 us (0.987)
  Pallas kernels: 69.9 us -> 69 us
    pallas_call x1, Pallas kernels: 69.3 us -> 68.5 us  [body(): pl.pallas_call(kernel, out_shape=(pltpu.VMEM((1, rows), jnp.float32), plt...]
where the time goes in v4:
time: 69.8 us; the launch traced here: 69.6 us
  Pallas kernels  69 us (99%)
    pallas_call x1, Pallas kernels, body(): pl.pallas_call(kernel, out_shape=(pltpu.VMEM((1, rows), jnp.float32), plt...  68.5 us

profile of v4, /device:TPU:2, one launch (start us, length us, event | category | flops | bytes accessed | tf_op | source)
XLA Modules:
  0.0 69.6 jit_solution(1105485235614308019)
XLA Ops:
  0.6 68.5 %shard_map.76 = (f32[1,128]{1,0:T(1,128)S(1)}, f32[1,128]{1,0:T(1,128)S(1)}) custom-call(f32[128,4096]{1,0:T(8,128)} %emb_ref.1, s32[1,128]{1,0:T(1,128)} %bitcast.6, s32[1,128]{1,0:T(1,128)} %bitcast.7, s32[1,256]{1,0:T(1,128)} %bitcast.4, s32[1,256]{1,0:T(1,128)} %bitcast.5), custom_call_target="tpu_custom_call" | custom-call | tf_op jit(solution)/shard_map/pallas_call | solution.py:271
  69.1 0.5 shard_map.77

commit v5 on v4

--- a/solution.py
+++ b/solution.py
@@ -37,6 +37,13 @@
     for i in [(dy * NX + dx) * NZ + dz]
     if i
 ]
+
+
+def hops(i):
+    return sum(min(d, n - d) for d, n in zip(OFFSETS[i], (NY, NX, NZ)))
+
+
+FAR_FIRST = sorted(ORDER, key=lambda i: -hops(i))
 SEMS = N // NZ + NZ
 
 
@@ -76,6 +83,9 @@
     me = lax.axis_index("dev")
     rows, width = raw.shape
     slots = packed.shape[0]
+    barrier = pltpu.get_barrier_semaphore()
+    for i in FAR_FIRST:
+        pl.semaphore_signal(barrier, inc=1, device_id={"dev": peer(me, i)}, device_id_type=MESH)
     pieces = 4
     step = rows // pieces
     smalls = []
@@ -91,9 +101,6 @@
         load = pltpu.make_async_copy(emb_ref.at[part], raw.at[part], load_sem.at[p])
         load.start()
         loads.append(load)
-    barrier = pltpu.get_barrier_semaphore()
-    for i in ORDER:
-        pl.semaphore_signal(barrier, inc=1, device_id={"dev": peer(me, i)}, device_id_type=MESH)
 
     for load in smalls:
         load.wait()
@@ -234,7 +241,7 @@
     answers[...] = jnp.where(lane < 64, halves[0], halves[1])
 
     back = (answers, returned, back_send, back_recv, functools.partial(source, me), 1)
-    exchange(*back)
+    exchange(*back, FAR_FIRST)
     own = pltpu.make_async_copy(answers.at[pl.ds(0, 1)], returned.at[pl.ds(0, 1)], own_sem)
     own.start()
     means = [
@@ -242,14 +249,15 @@
         for b in range(2)
     ]
     mean_ref[...] = jnp.where(lane == 0, means[0], means[1])
+    offset = lax.broadcasted_iota(jnp.int32, (N, rows), 0)
+    goal = shifted(me, offset // (NX * NZ), offset // NZ % NX, offset % NZ)
+    mine = [slot_row == 2 * goal + b for b in range(2)]
     own.wait()
     for copy in waits(*back):
         copy.wait_recv()
-    offset = lax.broadcasted_iota(jnp.int32, (N, rows), 0)
-    goal = shifted(me, offset // (NX * NZ), offset // NZ % NX, offset % NZ)
     row_best = jnp.full((1, rows), -2.0, jnp.float32)
     for b in range(2):
-        found = jnp.where(slot_row == 2 * goal + b, returned[:, 64 * b:64 * b + 1], -2.0)
+        found = jnp.where(mine[b], returned[:, 64 * b:64 * b + 1], -2.0)
         row_best = jnp.maximum(row_best, jnp.max(found, axis=0, keepdims=True))
     best_ref[...] = row_best
     for copy in (*waits(*there), *waits(*back), *speak, *forward):

time: 69.8 us -> 69.4 us (level)
  no operation moved by 1% of the time
where the time goes in v5:
time: 69.4 us; the launch traced here: 69.3 us
  Pallas kernels  68.6 us (99%)
    pallas_call x1, Pallas kernels, body(): pl.pallas_call(kernel, out_shape=(pltpu.VMEM((1, rows), jnp.float32), plt...  68.1 us

profile of v5, /device:TPU:2, one launch (start us, length us, event | category | flops | bytes accessed | tf_op | source)
XLA Modules:
  0.0 69.3 jit_solution(6870556029944266002)
XLA Ops:
  0.6 68.1 %shard_map.76 = (f32[1,128]{1,0:T(1,128)S(1)}, f32[1,128]{1,0:T(1,128)S(1)}) custom-call(f32[128,4096]{1,0:T(8,128)} %emb_ref.1, s32[1,128]{1,0:T(1,128)} %bitcast.6, s32[1,128]{1,0:T(1,128)} %bitcast.7, s32[1,256]{1,0:T(1,128)} %bitcast.4, s32[1,256]{1,0:T(1,128)} %bitcast.5), custom_call_target="tpu_custom_call" | custom-call | tf_op jit(solution)/shard_map/pallas_call | solution.py:279
  68.8 0.5 shard_map.77

commit v6 on v5

--- a/solution.py
+++ b/solution.py
@@ -31,8 +31,9 @@
 
 ORDER = [
     i
-    for dy in (2, 3, 1, 0)
+    for dys in ((2, 3), (1,), (0,))
     for dx in (2, 1, 3, 0)
+    for dy in dys
     for dz in (4, 3, 5, 2, 6, 1, 7, 0)
     for i in [(dy * NX + dx) * NZ + dz]
     if i
@@ -185,14 +186,10 @@
             copy.wait_recv()
 
     def gram(start, count, start_j, count_j):
-        total = jnp.zeros((count, count_j), jnp.float32)
-        chunk = 1024
-        for k in range(0, width, chunk):
-            total += lax.dot_general(
-                got[start:start + count, k:k + chunk], got[start_j:start_j + count_j, k:k + chunk],
-                (((1,), (1,)), ((), ())), preferred_element_type=jnp.float32,
-            )
-        return total
+        return lax.dot_general(
+            got[start:start + count, :], got[start_j:start_j + count_j, :],
+            (((1,), (1,)), ((), ())), preferred_element_type=jnp.float32,
+        )
 
     def rows_of(start, count):
         rank = ranks[start:start + count, 0:1]

time: 69.4 us -> 69.4 us (level)
  no operation moved by 1% of the time
where the time goes in v6:
time: 69.4 us; the launch traced here: 69.3 us
  Pallas kernels  68.6 us (99%)
    pallas_call x1, Pallas kernels, body(): pl.pallas_call(kernel, out_shape=(pltpu.VMEM((1, rows), jnp.float32), plt...  68.1 us

profile of v6, /device:TPU:2, one launch (start us, length us, event | category | flops | bytes accessed | tf_op | source)
XLA Modules:
  0.0 69.3 jit_solution(774194901353572837)
XLA Ops:
  0.6 68.1 %shard_map.76 = (f32[1,128]{1,0:T(1,128)S(1)}, f32[1,128]{1,0:T(1,128)S(1)}) custom-call(f32[128,4096]{1,0:T(8,128)} %emb_ref.1, s32[1,128]{1,0:T(1,128)} %bitcast.6, s32[1,128]{1,0:T(1,128)} %bitcast.7, s32[1,256]{1,0:T(1,128)} %bitcast.4, s32[1,256]{1,0:T(1,128)} %bitcast.5), custom_call_target="tpu_custom_call" | custom-call | tf_op jit(solution)/shard_map/pallas_call | solution.py:276
  68.7 0.5 shard_map.77
